TPU v7x, 8 devices: a whole 2x2x1 slice. The times are simulated.
8 devices in a mesh: dp: 2 (over y, z), tp: 4 (over x, core).
Axes of the slice: x: 2, y: 2, z: 1, core: 2. Of those that a mesh axis runs over, the one named last changes fastest.
Arguments:
- x: bfloat16 [4096, 2048], P('dp'), parts along dimension 0
- dy: bfloat16 [4096, 2048], P('dp'), parts along dimension 0
- gate: bfloat16 [4096, 6144], P('dp', 'tp'), parts along dimension 0
- up: bfloat16 [4096, 6144], P('dp', 'tp'), parts along dimension 0
- w_gate: bfloat16 [2048, 6144], P(None, 'tp')
- w_up: bfloat16 [2048, 6144], P(None, 'tp')
- w_down: bfloat16 [6144, 2048], P('tp')
Outputs:
- output 1: bfloat16 [4096, 2048], P('dp'), parts along dimension 0
- output 2: bfloat16 [4096, 6144], P('dp', 'tp'), parts along dimension 0
- output 3: bfloat16 [4096, 6144], P('dp', 'tp'), parts along dimension 0
- output 4: bfloat16 [12288, 2048], P(('dp', 'tp')), parts along dimension 0
There are 2 independent parts. A program takes and returns all parts, laid end to end along the dimension named above; an argument that names none is the same for every part.
All inputs are finite; a program needn't handle non-finite values.
Results may differ from a plain program's by a relative error of at most 0.012.
Values are sent between devices in bfloat16 or wider.
A program may use at most 2 GiB of HBM per device.

v0:
```python
import jax
import jax.numpy as jnp
from jax import lax
from jax.sharding import PartitionSpec as P


def act(gate, up):
    return jax.nn.silu(gate) * up


def solution(mesh):
    def step(x, dy, gate, up, w_gate, w_up, w_down):
        hidden, back = jax.vjp(act, gate.astype(jnp.float32), up.astype(jnp.float32))
        d_hidden = jnp.dot(dy, w_down.T, preferred_element_type=jnp.float32)
        d_gate, d_up = (g.astype(jnp.bfloat16) for g in back(d_hidden))
        term = jnp.dot(d_gate, w_gate.T, preferred_element_type=jnp.float32) + jnp.dot(d_up, w_up.T, preferred_element_type=jnp.float32)
        dx = lax.psum(term.astype(jnp.bfloat16), "tp")
        dw_gate = jnp.dot(x.T, d_gate, preferred_element_type=jnp.float32)
        dw_up = jnp.dot(x.T, d_up, preferred_element_type=jnp.float32)
        dw_down = jnp.dot(hidden.astype(jnp.bfloat16).T, dy, preferred_element_type=jnp.float32)
        return dx, *(g.astype(jnp.bfloat16) for g in (dw_gate, dw_up, dw_down))

    tokens, columns, rows = P("dp", None), P(None, "tp"), P("tp", None)
    return jax.shard_map(
        step,
        mesh=mesh,
        in_specs=(tokens, tokens, P("dp", "tp"), P("dp", "tp"), columns, columns, rows),
        out_specs=(tokens, P("dp", "tp"), P("dp", "tp"), P(("dp", "tp"), None)),
        check_vma=False,
    )
```

profile of v0, /device:TPU:0, one launch (start us, length us, event | category | flops | bytes accessed | tf_op | source)
XLA Modules:
  0.0 242.4 jit_solution(11695839772969577975)
XLA Ops:
  7.2 0.0 all-reduce.2.cloned.1.call-start
  7.2 28.6 %multiply_convert_fusion = (bf16[2048,1536]{1,0:T(8,128)(2,1)}, bf16[2048,1536]{1,0:T(8,128)(2,1)}) fusion(bf16[2048,1536]{1,0:T(8,128)(2,1)} %param.9, bf16[2048,1536]{1,0:T(8,128)(2,1)} %param.10, bf16[2048,2048]{1,0:T(8,128)(2,1)} %param.8, bf16[1536,2048]{1,0:T(8,128)(2,1)} %param.13), kind=kOutput, calls=%fused_computation.14 | convolution fusion | flops 12935233536 | bytes 39845888 | tf_op jit(solution)/shard_map/dot_general | solution.py:14
  35.8 19.5 %fusion.11 = f32[2048,2048]{1,0:T(8,128)} fusion(bf16[2048,1536]{1,0:T(8,128)(2,1)} %get-tuple-element.9, bf16[2048,1536]{1,0:T(8,128)(2,1)} %param.11), kind=kOutput, calls=%fused_computation.21 | convolution fusion | flops 12884901888 | bytes 29360128 | tf_op jit(solution)/shard_map/dot_general | solution.py:16
  55.3 21.7 %add_convert_fusion = bf16[2048,2048]{1,0:T(8,128)(2,1)} fusion(f32[2048,2048]{1,0:T(8,128)} %fusion.11, bf16[2048,1536]{1,0:T(8,128)(2,1)} %get-tuple-element.8, bf16[2048,1536]{1,0:T(8,128)(2,1)} %param.12), kind=kOutput, calls=%fused_computation.4 | convolution fusion | flops 12893290496 | bytes 37748736 | tf_op jit(solution)/shard_map/dot_general | solution.py:16
  76.9 0.0 slice-start
  76.9 0.0 all-reduce.2.cloned.1.call-update
  77.0 0.0 slice-start.1
  77.0 19.3 %fusion.7 = bf16[2048,1536]{0,1:T(8,128)(2,1)} fusion(bf16[2048,1536]{1,0:T(8,128)(2,1)} %get-tuple-element.9, bf16[2048,2048]{1,0:T(8,128)(2,1)} %param.7), kind=kOutput, calls=%fused_computation.18 | convolution fusion | flops 12888047616 | bytes 20971520 | tf_op jit(solution)/shard_map/dot_general | solution.py:18
  96.2 0.0 slice-done
  96.2 0.0 slice-done.1
  96.3 17.6 %fusion.8 = bf16[2048,1536]{0,1:T(8,128)(2,1)} fusion(bf16[2048,1536]{1,0:T(8,128)(2,1)S(1)} %bitcast.16, bf16[2048,2048]{1,0:T(8,128)(2,1)} %param.7), kind=kOutput, calls=%fused_computation.19 | convolution fusion | flops 12888047616 | bytes 20971520 | tf_op jit(solution)/shard_map/dot_general | solution.py:19
  113.8 8.6 %copy.11 = bf16[2048,1536]{1,0:T(8,128)(2,1)} copy(bf16[2048,1536]{0,1:T(8,128)(2,1)} %fusion.7) | data formatting | bytes 12582912
  122.4 8.6 %copy.12 = bf16[2048,1536]{1,0:T(8,128)(2,1)} copy(bf16[2048,1536]{0,1:T(8,128)(2,1)} %fusion.8) | data formatting | bytes 12582912
  131.1 21.4 %convolution_convert_fusion = bf16[1536,2048]{1,0:T(8,128)(2,1)} fusion(bf16[2048,2048]{1,0:T(8,128)(2,1)} %param.8, bf16[2048,1536]{1,0:T(8,128)(2,1)} %param.10, bf16[2048,1536]{1,0:T(8,128)(2,1)} %param.9), kind=kOutput, calls=%fused_computation.15 | convolution fusion | flops 12913213440 | bytes 27262976 | tf_op jit(solution)/shard_map/dot_general | solution.py:20
  152.5 74.6 %all-reduce.2.cloned.1.call-done = bf16[2048,2048]{1,0:T(8,128)(2,1)} async-done(((bf16[2048,2048]{1,0:T(8,128)(2,1)}), bf16[2048,2048]{1,0:T(8,128)(2,1)}) %all-reduce.2.cloned.1.call-update) | async-done | bytes 8388624 | tf_op jit(solution)/shard_map/psum | solution.py:17
  227.1 8.4 %copy.14 = bf16[2048,2048]{1,0:T(8,128)(2,1)} copy(bf16[2048,2048]{1,0:T(8,128)(2,1)} %all-reduce.2.cloned.1.call-done) | data formatting | bytes 16777216
  (1 shorter events, 0.0 us)
Async XLA Ops:
  7.2 219.9 %all-reduce.2.cloned.1.call-start = ((), (), s32[]{:S(2)}) async-start(), calls=%async_computation | async-start | bytes 16777216 | tf_op jit(solution)/shard_map/psum | solution.py:17
  76.9 19.3 %slice-start = ((s8[6291456]{0:T(1024)(128)(4,1)}), s8[2097152]{0:T(1024)(128)(4,1)S(1)}, s32[]{:S(2)}) async-start(s8[6291456]{0:T(1024)(128)(4,1)} %bitcast.15), calls=%async_computation.1 | async-start | bytes 4194304
  77.0 19.3 %slice-start.1 = ((s8[6291456]{0:T(1024)(128)(4,1)}), s8[4194304]{0:T(1024)(128)(4,1)S(1)}, s32[]{:S(2)}) async-start(s8[6291456]{0:T(1024)(128)(4,1)} %bitcast.15), calls=%async_computation.2 | async-start | bytes 8388608
Sparse Core Ops, SparseCore 0:
  77.1 149.9 all-reduce.1
where the time goes:
time: 243 us; the launch traced here: 242 us
  matrix products  128 us (53%)
  waiting for transfers between devices  74.6 us (31%)
  local copies, waits for them, and re-layouts  25.7 us (11%)
  between operations  14 us (6%)
    psum x1, waiting for transfers between devices, step(): dx = lax.psum(term.astype(jnp.bfloat16), 'tp')  74.6 us
    dot_general x1, matrix products, step(): d_hidden = jnp.dot(dy, w_down.T, preferred_element_type=jnp.float32)  28.6 us
    unnamed x7, local copies, waits for them, and re-layouts  25.7 us
    dot_general x1, matrix products, step(): jnp.dot(d_up, w_up.T, preferred_element_type=jnp.float32)  21.7 us
    dot_general x1, matrix products, step(): jnp.dot(hidden.astype(jnp.bfloat16).T, dy, preferred_element_type=jnp.flo...  21.4 us
    dot_general x1, matrix products, step(): jnp.dot(d_gate, w_gate.T, preferred_element_type=jnp.float32)  19.5 us
    dot_general x1, matrix products, step(): dw_gate = jnp.dot(x.T, d_gate, preferred_element_type=jnp.float32)  19.3 us
    dot_general x1, matrix products, step(): dw_up = jnp.dot(x.T, d_up, preferred_element_type=jnp.float32)  17.6 us
  transfers between devices with their start and end apart: 1, of which 1 were waited for; matrix products, arithmetic and copies ran while one was open for 31% of the time, Pallas kernels for 0%

commit v1 on v0

v1 whole, which is shorter than its diff:
```python
import functools

import jax
import jax.numpy as jnp
from jax import lax
from jax.experimental import pallas as pl
from jax.experimental.pallas import tpu as pltpu
from jax.sharding import PartitionSpec as P


MESH = pl.DeviceIdType.MESH
BF16, F32 = jnp.bfloat16, jnp.float32
ANY = pl.BlockSpec(memory_space=pl.ANY)
MIB = 2**20

ROWS, D, FF = 2048, 2048, 1536
HALF = D // 2
RB = 256
NB = ROWS // RB
HB = RB // 2
NX = 10
PARTS = ((10, 15), (15, 16))
TILE = 512
Q = 512
NQ = HALF // Q
BX = 512
NJ = D // BX
BH = FF // NJ

CHIPS = [(0, 2), (2, 0), (1, 3), (3, 1)]
CORES = [(0, 1), (1, 0), (2, 3), (3, 2)]


def dot(a, b, dims):
    return lax.dot_general(a, b, (dims, ((), ())), preferred_element_type=F32)


def to(axis, index):
    return dict(device_id={axis: index}, device_id_type=MESH)


def term_kernel(dy, gate, up, wd, wg, wu, x, du_o, h_o, dwg_o, dxp, *refs):
    n = len(PARTS)
    own_o, both_o, refs = refs[:n], refs[n : 2 * n], refs[2 * n :]
    (
        wd_v, wgu_v, dy_v, ga_v, up_v, dgu_v, h_v, dg_v, x_v, yours, mine, theirs, s_v, q_v, f_v,
        yours_0, theirs_0, s_0, q_0, f_0,
        wd_sem, wg_sem, in_sem, out_sem, x_sem, dw_sem, cs_sem, cr_sem, xs_sem, xr_sem, gs_sem, gr_sem, f_sem,
        own_sem, both_sem, bs_sem, br_sem, cs0, cr0, xs0, xr0, gs0, gr0, f0,
    ) = refs
    me = lax.axis_index("tp")
    core = lax.rem(me, 2)
    partner = me + 1 - 2 * core
    across = lax.rem(me + 2, 4)

    def rows(i):
        return pl.ds(pl.multiple_of(i * RB, RB), RB)

    def loads(i, slot):
        return [
            pltpu.make_async_copy(src.at[rows(i)], dst.at[slot], in_sem.at[n, slot])
            for n, (src, dst) in enumerate(((dy, dy_v), (gate, ga_v), (up, up_v)))
        ]

    def stores(i, slot):
        return [
            pltpu.make_async_copy(dgu_v.at[slot, :, pl.ds(FF, FF)], du_o.at[rows(i)], out_sem.at[0, slot]),
            pltpu.make_async_copy(h_v.at[slot], h_o.at[rows(i)], out_sem.at[1, slot]),
        ]

    def swap(i):
        return pltpu.make_async_remote_copy(
            yours.at[i], theirs.at[i], cs_sem.at[i], cr_sem.at[i], **to("tp", partner)
        )

    def cross(k):
        return pltpu.make_async_remote_copy(s_v.at[k], q_v.at[k], xs_sem.at[k], xr_sem.at[k], **to("tp", across))

    def finished(k):
        return dxp.at[core, pl.ds(pl.multiple_of(k * HB, HB), HB)]

    def keep(k):
        return pltpu.make_async_copy(f_v.at[k], finished(k), f_sem.at[k])

    def give(k):
        return pltpu.make_async_remote_copy(f_v.at[k], finished(k), gs_sem.at[k], gr_sem.at[k], **to("tp", partner))

    def swap_0(q):
        return pltpu.make_async_remote_copy(yours_0.at[q], theirs_0.at[q], cs0.at[q], cr0.at[q], **to("tp", partner))

    def cross_0(q):
        return pltpu.make_async_remote_copy(s_0.at[q], q_0.at[q], xs0.at[q], xr0.at[q], **to("tp", across))

    def finished_0(q):
        return dxp.at[core, pl.ds(0, RB), pl.ds(pl.multiple_of(q * Q, Q), Q)]

    def keep_0(q):
        return pltpu.make_async_copy(f_0.at[q], finished_0(q), f0.at[q])

    def give_0(q):
        return pltpu.make_async_remote_copy(f_0.at[q], finished_0(q), gs0.at[q], gr0.at[q], **to("tp", partner))

    def hand_on(k):
        for own, both, (first, last) in zip(own_o, both_o, PARTS):
            if first <= k < last:
                at, j = pl.ds((k - first) * HB, HB), k - NX
                return (
                    pltpu.make_async_copy(s_v.at[k], own.at[at], own_sem.at[j]),
                    pltpu.make_async_copy(s_v.at[k], both.at[core, at], both_sem.at[j]),
                    pltpu.make_async_remote_copy(
                        s_v.at[k], both.at[core, at], bs_sem.at[j], br_sem.at[j], **to("tp", partner)
                    ),
                )

    def wd_load(t):
        at = pl.ds(t * TILE, TILE)
        return pltpu.make_async_copy(wd.at[at], wd_v.at[at], wd_sem.at[t])

    def wgu_at(half, t, size):
        return pl.ds(pl.multiple_of(half * HALF + t * size, size), size)

    def wgu_load(n, half, t):
        at = wgu_at(half, t, Q)
        return [
            pltpu.make_async_copy(w.at[at], wgu_v.at[at, pl.ds(m * FF, FF)], wg_sem.at[n, t, m])
            for m, w in enumerate((wg, wu))
        ]

    def x_at(j):
        return x_v if j == 0 else wgu_v.at[:, pl.ds((j - 1) * BX, BX)]

    def x_load(j):
        return pltpu.make_async_copy(x.at[:, pl.ds(j * BX, BX)], x_at(j), x_sem.at[j])

    def dw_at(j):
        return wgu_v.at[pl.ds(j * BX, BX), pl.ds(FF, FF)]

    def dw_store(j):
        return pltpu.make_async_copy(dw_at(j), dwg_o.at[pl.ds(j * BX, BX)], dw_sem.at[j])

    def start(copies):
        for copy in copies:
            copy.start()

    def wait(copies):
        for copy in copies:
            copy.wait()

    first_loads = loads(0, 0)
    start([first_loads[0], wd_load(0)])
    start([*first_loads[1:], wd_load(1)])

    barrier = pltpu.get_barrier_semaphore()
    for other in (partner, across):
        pl.semaphore_signal(barrier, inc=1, **to("tp", other))
    pl.semaphore_wait(barrier, 2)

    def finish(k):
        cross(k).wait_recv()
        f_v[k] = (s_v[k].astype(F32) + q_v[k].astype(F32)).astype(BF16)
        keep(k).start()
        give(k).start()

    def finish_0(q):
        cross_0(q).wait_recv()
        f_0[q] = (s_0[q].astype(F32) + q_0[q].astype(F32)).astype(BF16)
        keep_0(q).start()
        give_0(q).start()

    def hidden(i, slot, t):
        cols = pl.ds(t * TILE, TILE)
        d_hidden = dot(dy_v[slot], wd_v[cols, :], ((1,), (1,)))
        if isinstance(i, int) and t == 0:
            wait(first_loads[1:])
        g, u = ga_v[slot, :, cols].astype(F32), up_v[slot, :, cols].astype(F32)
        sig = jax.nn.sigmoid(g)
        silu = g * sig
        d_gate = (d_hidden * u * (sig + silu * (1.0 - sig))).astype(BF16)
        h_v[slot, :, cols] = (silu * u).astype(BF16)
        dgu_v[slot, :, cols] = d_gate
        dg_v[rows(i), cols] = d_gate
        dgu_v[slot, :, pl.ds(FF + t * TILE, TILE)] = (d_hidden * silu).astype(BF16)

    def term(slot, half, t, size):
        return dot(dgu_v[slot], wgu_v[wgu_at(half, t, size), :], ((1,), (1,)))

    def first_block():
        wait([first_loads[0], wd_load(0)])
        start([wd_load(2)])
        hidden(0, 0, 0)
        wait([wd_load(1)])
        halves = (1 - core, core)
        order = [(n, half, q) for q in range(NQ) for n, half in enumerate(halves)]
        start(wgu_load(*order[0]))
        hidden(0, 0, 1)
        wait([wd_load(2)])
        start(wgu_load(*order[1]))
        start(wgu_load(*order[2]))
        hidden(0, 0, 2)

        def add(q):
            swap_0(q).wait_recv()
            at = pl.ds(q * Q, Q)
            s_0[q] = (mine[:, at] + theirs_0[q].astype(F32)).astype(BF16)
            cross_0(q).start()

        for at, (n, half, q) in enumerate(order):
            wait(wgu_load(n, half, q))
            if at + 3 < len(order):
                start(wgu_load(*order[at + 3]))
            elif at + 3 == len(order):
                start(loads(1, 1))
            elif at + 3 == len(order) + 1:
                start(stores(0, 0))
            got = term(0, half, q, Q)
            if n == 0:
                yours_0[q] = got.astype(BF16)
                swap_0(q).start()
            else:
                mine[:, pl.ds(q * Q, Q)] = got
                if q:
                    add(q - 1)
        add(NQ - 1)

    def block(i):
        slot = lax.rem(i, 2)
        wait(loads(i, slot))

        @pl.when(i + 1 < NB)
        def _():
            start(loads(i + 1, 1 - slot))

        @pl.when(i == 1)
        def _():
            x_load(0).start()

        @pl.when(i >= 2)
        def _():
            wait(stores(i - 2, slot))

        for t in range(FF // TILE):
            hidden(i, slot, t)
        start(stores(i, slot))

        for t in range(HALF // TILE):
            yours[i, :, pl.ds(t * TILE, TILE)] = term(slot, 1 - core, t, TILE).astype(BF16)
        swap(i).start()
        for t in range(HALF // TILE):
            mine[:, pl.ds(t * TILE, TILE)] = term(slot, core, t, TILE)
        swap(i).wait_recv()
        for n in range(2):
            part = pl.ds(n * HB, HB)
            s_v[2 * i + n] = (mine[part, :] + theirs[i, part, :].astype(F32)).astype(BF16)

            @pl.when(2 * i + n < NX)
            def _():
                cross(2 * i + n).start()

        for k in range(NX, 2 * NB):

            @pl.when(i == k // 2)
            def _():
                start(hand_on(k))

        @pl.when(i <= 2)
        def _():
            finish_0(i - 1)

        @pl.when(i >= 4)
        def _():
            finish(i - 2)

    def step(i, carry):
        block(i)
        return carry

    first_block()
    lax.fori_loop(1, NB, step, 0)

    for j in range(1, NJ):
        x_load(j).start()
    late = {0: (NB - 2,), 1: (NB - 1,), 3: tuple(range(NB, NX))}
    for j in range(NJ):
        x_load(j).wait()
        dw_at(j)[...] = dot(x_at(j)[...], dg_v[...], ((0,), (0,))).astype(BF16)
        dw_store(j).start()
        for k in late.get(j, ()):
            finish(k)

    for i in (NB - 2, NB - 1):
        wait(stores(i, i % 2))
    for i in range(1, NB):
        swap(i).wait_send()
    for k in range(NX, 2 * NB):
        wait(hand_on(k))
    for j in range(NJ):
        dw_store(j).wait()
    for q in range(NQ):
        swap_0(q).wait_send()
        cross_0(q).wait_send()
        keep_0(q).wait()
        give_0(q).wait()
    for k in range(2, NX):
        cross(k).wait_send()
        keep(k).wait()
        give(k).wait()


def terms(dy, gate, up, w_down, w_gate, w_up, x):
    hidden = jax.ShapeDtypeStruct((ROWS, FF), BF16)
    dma = pltpu.SemaphoreType.DMA
    late = 2 * NB - NX
    return pl.pallas_call(
        term_kernel,
        name="terms",
        out_shape=(
            hidden,
            hidden,
            jax.ShapeDtypeStruct((D, FF), BF16),
            jax.ShapeDtypeStruct((2, NX * HB, HALF), BF16),
            *(jax.ShapeDtypeStruct(((b - a) * HB, HALF), BF16) for a, b in PARTS),
            *(jax.ShapeDtypeStruct((2, (b - a) * HB, HALF), BF16) for a, b in PARTS),
        ),
        in_specs=[ANY] * 7,
        out_specs=(ANY,) * (4 + 2 * len(PARTS)),
        scratch_shapes=[
            pltpu.VMEM((FF, D), BF16),
            pltpu.VMEM((D, 2 * FF), BF16),
            pltpu.VMEM((2, RB, D), BF16),
            pltpu.VMEM((2, RB, FF), BF16),
            pltpu.VMEM((2, RB, FF), BF16),
            pltpu.VMEM((2, RB, 2 * FF), BF16),
            pltpu.VMEM((2, RB, FF), BF16),
            pltpu.VMEM((ROWS, FF), BF16),
            pltpu.VMEM((ROWS, BX), BF16),
            pltpu.VMEM((NB, RB, HALF), BF16),
            pltpu.VMEM((RB, HALF), F32),
            pltpu.VMEM((NB, RB, HALF), BF16),
            pltpu.VMEM((2 * NB, HB, HALF), BF16),
            pltpu.VMEM((NX, HB, HALF), BF16),
            pltpu.VMEM((NX, HB, HALF), BF16),
            *(pltpu.VMEM((NQ, RB, Q), BF16) for _ in range(5)),
            dma((FF // TILE,)),
            dma((2, NQ, 2)),
            dma((3, 2)),
            dma((2, 2)),
            dma((NJ,)),
            dma((NJ,)),
            *(dma((NB,)) for _ in range(2)),
            *(dma((NX,)) for _ in range(5)),
            *(dma((late,)) for _ in range(4)),
            *(dma((NQ,)) for _ in range(7)),
        ],
        cost_estimate=pl.CostEstimate(flops=8 * ROWS * D * FF, bytes_accessed=60 * MIB, transcendentals=ROWS * FF),
        compiler_params=pltpu.CompilerParams(collective_id=0, has_side_effects=True, vmem_limit_bytes=62 * MIB),
    )(dy, gate, up, w_down, w_gate, w_up, x)


def weight_kernel(
    x, h, du, dy, dwg_t, dxp, dwg, dwu, dwd, dx,
    x_v, h_v, du_v, dy_v, ou_v, od_v, dwg_v, dx_v, x_sem, h_sem, du_sem, dy_sem, ou_sem, od_sem, take_sem, put_sem,
):
    j = pl.program_id(0)
    slot = lax.rem(j, 2)

    def x_load(j, slot):
        at = pl.ds(pl.multiple_of(j * BX, BX), BX)
        return pltpu.make_async_copy(x.at[:, at], x_v.at[slot], x_sem.at[slot])

    def du_load(t):
        at = pl.ds(t * TILE, TILE)
        return pltpu.make_async_copy(du.at[:, at], du_v.at[:, at], du_sem.at[t])

    def store(src, dst, size, j, sem):
        return pltpu.make_async_copy(src, dst.at[pl.ds(pl.multiple_of(j * size, size), size)], sem)

    def put_up(j, slot):
        return store(ou_v.at[slot], dwu, BX, j, ou_sem.at[slot])

    def put_down(j, slot):
        return store(od_v.at[slot], dwd, BH, j, od_sem.at[slot])

    h_load = pltpu.make_async_copy(h, h_v, h_sem)
    dy_load = pltpu.make_async_copy(dy, dy_v, dy_sem)
    takes = [pltpu.make_async_copy(dxp.at[c], dx_v.at[:, pl.ds(c * HALF, HALF)], take_sem.at[c]) for c in range(2)]
    takes.append(pltpu.make_async_copy(dwg_t, dwg_v, take_sem.at[2]))
    puts = [
        pltpu.make_async_copy(dx_v, dx.at[pl.ds(0, NX * HB)], put_sem.at[0]),
        pltpu.make_async_copy(dwg_v, dwg, put_sem.at[1]),
    ]

    @pl.when(j == 0)
    def _():
        x_load(0, 0).start()
        du_load(0).start()
        x_load(0, 0).wait()
        du_load(1).start()
        for t in range(FF // TILE):
            at = pl.ds(t * TILE, TILE)
            du_load(t).wait()
            if t + 2 < FF // TILE:
                du_load(t + 2).start()
            else:
                if t + 2 == FF // TILE:
                    x_load(1, 1).start()
            ou_v[0, :, at] = dot(x_v[0], du_v[:, at], ((0,), (0,))).astype(BF16)
        put_up(0, 0).start()

    @pl.when(jnp.logical_and(j > 0, j < NJ))
    def _():
        x_load(j, slot).wait()

        @pl.when(j + 1 < NJ)
        def _():
            x_load(j + 1, 1 - slot).start()

        @pl.when(j == 1)
        def _():
            h_load.start()

        @pl.when(j == 2)
        def _():
            dy_load.start()

        @pl.when(j == 3)
        def _():
            for copy in takes:
                copy.start()

        @pl.when(j >= 2)
        def _():
            put_up(j - 2, slot).wait()

        ou_v[slot] = dot(x_v[slot], du_v[...], ((0,), (0,))).astype(BF16)
        put_up(j, slot).start()

    @pl.when(j == NJ)
    def _():
        h_load.wait()
        dy_load.wait()

    @pl.when(j == NJ + 1)
    def _():
        for copy in takes:
            copy.wait()
        for copy in puts:
            copy.start()

    @pl.when(j >= NJ)
    def _():
        k = j - NJ

        @pl.when(k >= 2)
        def _():
            put_down(k - 2, slot).wait()

        od_v[slot] = dot(h_v[:, pl.ds(pl.multiple_of(k * BH, BH), BH)], dy_v[...], ((0,), (0,))).astype(BF16)
        put_down(k, slot).start()

    @pl.when(j == 2 * NJ - 1)
    def _():
        for copy in puts:
            copy.wait()
        for k in (NJ - 2, NJ - 1):
            put_up(k, k % 2).wait()
            put_down(k, k % 2).wait()


def weights(x, h, du, dy, dwg_t, dxp):
    dma = pltpu.SemaphoreType.DMA
    return pl.pallas_call(
        weight_kernel,
        name="weights",
        grid=(2 * NJ,),
        out_shape=(
            jax.ShapeDtypeStruct((D, FF), BF16),
            jax.ShapeDtypeStruct((D, FF), BF16),
            jax.ShapeDtypeStruct((FF, D), BF16),
            jax.ShapeDtypeStruct((ROWS, D), BF16),
        ),
        in_specs=[ANY] * 6,
        out_specs=(ANY,) * 4,
        scratch_shapes=[
            pltpu.VMEM((2, ROWS, BX), BF16),
            pltpu.VMEM((ROWS, FF), BF16),
            pltpu.VMEM((ROWS, FF), BF16),
            pltpu.VMEM((ROWS, D), BF16),
            pltpu.VMEM((2, BX, FF), BF16),
            pltpu.VMEM((2, BH, D), BF16),
            pltpu.VMEM((D, FF), BF16),
            pltpu.VMEM((NX * HB, D), BF16),
            dma((2,)),
            dma,
            dma((FF // TILE,)),
            dma,
            dma((2,)),
            dma((2,)),
            dma((3,)),
            dma((2,)),
        ],
        cost_estimate=pl.CostEstimate(flops=4 * ROWS * D * FF, bytes_accessed=60 * MIB, transcendentals=0),
        compiler_params=pltpu.CompilerParams(vmem_limit_bytes=60 * MIB),
    )(x, h, du, dy, dwg_t, dxp)


def place_kernel(first, both, own, other, dx, out, both_v, own_v, other_v, out_v, in_sem, out_sem):
    core = lax.rem(lax.axis_index("tp"), 2)
    n = own.shape[0] // HB

    def loads(k):
        at = pl.ds(k * HB, HB)
        return [
            pltpu.make_async_copy(both.at[:, at], both_v.at[:, at], in_sem.at[0, k]),
            pltpu.make_async_copy(own.at[at], own_v.at[at], in_sem.at[1, k]),
            pltpu.make_async_copy(other.at[at], other_v.at[at], in_sem.at[2, k]),
        ]

    def store(k):
        return pltpu.make_async_copy(
            out_v.at[pl.ds(k * HB, HB)], out.at[pl.ds((first + k) * HB, HB)], out_sem.at[k]
        )

    for k in range(n):
        for copy in loads(k):
            copy.start()
    for k in range(n):
        at = pl.ds(k * HB, HB)
        for copy in loads(k):
            copy.wait()
        for c in range(2):

            @pl.when(core == c)
            def _():
                for half, q in ((c, own_v), (1 - c, other_v)):
                    total = both_v[half, at].astype(F32) + q[at].astype(F32)
                    out_v[at, half * HALF : (half + 1) * HALF] = total.astype(BF16)

        store(k).start()
    for k in range(n):
        store(k).wait()


def place(dx, both, own, other, first):
    rows = own.shape[0]
    n = rows // HB
    return pl.pallas_call(
        functools.partial(place_kernel, first),
        name="place",
        out_shape=jax.ShapeDtypeStruct(dx.shape, BF16),
        in_specs=[ANY] * 4,
        out_specs=ANY,
        scratch_shapes=[
            pltpu.VMEM((2, rows, HALF), BF16),
            pltpu.VMEM((rows, HALF), BF16),
            pltpu.VMEM((rows, HALF), BF16),
            pltpu.VMEM((rows, D), BF16),
            pltpu.SemaphoreType.DMA((3, n)),
            pltpu.SemaphoreType.DMA((n,)),
        ],
        input_output_aliases={3: 0},
        cost_estimate=pl.CostEstimate(flops=rows * D, bytes_accessed=rows * D * 6, transcendentals=0),
        compiler_params=pltpu.CompilerParams(vmem_limit_bytes=16 * MIB),
    )(both, own, other, dx)


def solution(mesh):
    def step(x, dy, gate, up, w_gate, w_up, w_down):
        du, h, dw_gate, dxp, *parts = terms(dy, gate, up, w_down, w_gate, w_up, x)
        own, both = parts[: len(PARTS)], parts[len(PARTS) :]
        crossed = []
        for part in own:
            crossed.append(lax.ppermute(part, "tp", CHIPS))
        dw_gate, dw_up, dw_down, dx = weights(x, h, du, dy, dw_gate, dxp)
        for (first, _), part, q in zip(PARTS, both, crossed):
            dx, q = lax.optimization_barrier((dx, q))
            near = lax.ppermute(q, "tp", CORES)
            dx = place(dx, part, q, near, first)
        return dx, dw_gate, dw_up, dw_down

    tokens, columns, rows = P("dp", None), P(None, "tp"), P("tp", None)
    return jax.shard_map(
        step,
        mesh=mesh,
        in_specs=(tokens, tokens, P("dp", "tp"), P("dp", "tp"), columns, columns, rows),
        out_specs=(tokens, P("dp", "tp"), P("dp", "tp"), P(("dp", "tp"), None)),
        check_vma=False,
    )
```

time: 243 us -> 117 us (0.48)
  matrix products: 128 us -> 0 us
  Pallas kernels: 0 us -> 107 us
  waiting for transfers between devices: 74.6 us -> 6.48 us
  local copies, waits for them, and re-layouts: 25.7 us -> 0.01 us
  between operations: 14 us -> 0.87 us
    dot_general x6 -> x0, matrix products: 128 us -> none  [the longest x1 28.6 us: step(): d_hidden = jnp.dot(dy, w_down.T, preferred_element_type=jnp.float32)]
    pallas_call x0 -> x4, Pallas kernels: none -> 107 us  [the longest x1 71.9 us: terms(): pl.pallas_call(term_kernel, name='terms', out_shape=(hidden, hidden, jax....]
    psum x1 -> x0, waiting for transfers between devices: 74.6 us -> none  [step(): dx = lax.psum(term.astype(jnp.bfloat16), 'tp')]
    unnamed x7 -> x4, local copies, waits for them, and re-layouts: 25.7 us -> 0.01 us
    ppermute x0 -> x4, waiting for transfers between devices: none -> 6.48 us  [the longest x2 3.8 us: step(): crossed.append(lax.ppermute(part, 'tp', CHIPS))]
  transfers between devices with their start and end apart: 1 -> 4, of which waited for: 1 -> 3; matrix products, arithmetic and copies ran while one was open for 31% -> 0% of each run, Pallas kernels for 0% -> 29%
where the time goes in v1:
time: 117 us; the launch traced here: 116 us
  Pallas kernels  107 us (91%)
  waiting for transfers between devices  6.48 us (6%)
  starting transfers between devices  1.93 us (2%)
    pallas_call x1, Pallas kernels, terms(): pl.pallas_call(term_kernel, name='terms', out_shape=(hidden, hidden, jax....  71.9 us
    pallas_call x1, Pallas kernels, weights(): pl.pallas_call(weight_kernel, name='weights', grid=(2 * NJ,), out_shape=(...  32.1 us
    ppermute x2, waiting for transfers between devices, step(): crossed.append(lax.ppermute(part, 'tp', CHIPS))  3.8 us
    pallas_call x2, Pallas kernels, place(): pl.pallas_call(functools.partial(place_kernel, first), name='place', out_...  3.17 us
    ppermute x2, waiting for transfers between devices, step(): near = lax.ppermute(q, 'tp', CORES)  2.69 us
  transfers between devices with their start and end apart: 4, of which 3 were waited for; matrix products, arithmetic and copies ran while one was open for 0% of the time, Pallas kernels for 29%

profile of v1, /device:TPU:0, one launch (start us, length us, event | category | flops | bytes accessed | tf_op | source)
XLA Modules:
  0.0 116.4 jit_solution(10791117761672172979)
XLA Ops:
  0.6 71.9 %terms.1 = (bf16[2048,1536]{1,0:T(8,128)(2,1)}, bf16[2048,1536]{1,0:T(8,128)(2,1)}, bf16[2048,1536]{1,0:T(8,128)(2,1)}, bf16[2,1280,1024]{2,1,0:T(8,128)(2,1)}, ...) custom-call(bf16[2048,2048]{1,0:T(8,128)(2,1)} %dy.3, ...), custom_call_target="tpu_custom_call" | custom-call | flops 51539607552 | bytes 62914560 | tf_op jit(solution)/shard_map/terms/pallas_call | solution.py:313
  72.5 0.0 collective-permute-start
  72.6 0.0 copy-start
  72.6 32.1 %weights.1 = (bf16[2048,1536]{1,0:T(8,128)(2,1)}, bf16[2048,1536]{1,0:T(8,128)(2,1)}, bf16[1536,2048]{1,0:T(8,128)(2,1)}, bf16[2048,2048]{1,0:T(8,128)(2,1)}) custom-call(bf16[2048,2048]{1,0:T(8,128)(2,1)} %x.3, bf16[2048,1536]{1,0:T(8,128)(2,1)} %get-tuple-element.22.h, bf16[2048,1536]{1,0:T(8,128)(2,1)} %get-tuple-element.23.du, bf16[2048,2048]{1,0:T(8,128)(2,1)} %dy.3, ...), custom_call_target="tpu_custom_call" | custom-call | flops 25769803776 | bytes 62914560 | tf_op jit(solution)/shard_map/weights/pallas_call | solution.py:471
  104.7 0.0 collective-permute-done.own
  104.7 0.4 collective-permute-start.1
  105.1 1.5 %collective-permute-start.2 = (bf16[128,1024]{1,0:T(8,128)(2,1)}, bf16[128,1024]{1,0:T(8,128)(2,1)S(1)}, u32[]{:S(2)}, u32[]{:S(2)}) collective-permute-start(bf16[128,1024]{1,0:T(8,128)(2,1)} %get-tuple-element.30), channel_id=1, source_target_pairs={{0,2},{2,0},{1,3},{3,1},{4,6},{6,4},{5,7},{7,5}} | collective-permute-start | bytes 786440 | tf_op jit(solution)/shard_map/ppermute | solution.py:572
  106.6 1.2 collective-permute-done.1.other
  107.7 0.0 copy-done
  107.7 0.0 copy-start.1
  107.7 2.1 %place.2.dx = bf16[2048,2048]{1,0:T(8,128)(2,1)} custom-call(bf16[2,640,1024]{2,1,0:T(8,128)(2,1)S(1)} %copy-done, bf16[640,1024]{1,0:T(8,128)(2,1)S(1)} %collective-permute-done.own, bf16[640,1024]{1,0:T(8,128)(2,1)S(1)} %collective-permute-done.1.other, bf16[2048,2048]{1,0:T(8,128)(2,1)} %get-tuple-element.29.dx), custom_call_target="tpu_custom_call", output_to_operand_aliasing={{}: (3, {})} | custom-call | flops 1310720 | bytes 7864320 | tf_op jit(solution)/shard_map/place/pallas_call | solution.py:546
  109.9 3.8 %collective-permute-done.2.own = bf16[128,1024]{1,0:T(8,128)(2,1)S(1)} collective-permute-done((bf16[128,1024]{1,0:T(8,128)(2,1)}, bf16[128,1024]{1,0:T(8,128)(2,1)S(1)}, u32[]{:S(2)}, u32[]{:S(2)}) %collective-permute-start.2) | collective-permute-done | bytes 262176 | tf_op jit(solution)/shard_map/ppermute | solution.py:572
  113.7 0.0 collective-permute-start.3
  113.7 1.5 %collective-permute-done.3.other = bf16[128,1024]{1,0:T(8,128)(2,1)S(1)} collective-permute-done((bf16[128,1024]{1,0:T(8,128)(2,1)S(1)}, bf16[128,1024]{1,0:T(8,128)(2,1)S(1)}, u32[]{:S(2)}, u32[]{:S(2)}) %collective-permute-start.3) | collective-permute-done | bytes 262176 | tf_op jit(solution)/shard_map/ppermute | solution.py:576
  115.2 0.0 copy-done.1
  115.2 1.0 place.3
Async XLA Ops:
  72.5 32.2 %collective-permute-start = (bf16[640,1024]{1,0:T(8,128)(2,1)}, bf16[640,1024]{1,0:T(8,128)(2,1)S(1)}, u32[]{:S(2)}, u32[]{:S(2)}) collective-permute-start(bf16[640,1024]{1,0:T(8,128)(2,1)} %get-tuple-element.27), channel_id=1, source_target_pairs={{0,2},{2,0},{1,3},{3,1},{4,6},{6,4},{5,7},{7,5}} | collective-permute-start | bytes 3932168 | tf_op jit(solution)/shard_map/ppermute | solution.py:572
  72.6 35.2 %copy-start = (bf16[2,640,1024]{2,1,0:T(8,128)(2,1)S(1)}, bf16[2,640,1024]{2,1,0:T(8,128)(2,1)}, u32[]{:S(2)}) copy-start(bf16[2,640,1024]{2,1,0:T(8,128)(2,1)} %get-tuple-element.21.both) | copy-start | bytes 7864324
  104.7 3.1 %collective-permute-start.1 = (bf16[640,1024]{1,0:T(8,128)(2,1)S(1)}, bf16[640,1024]{1,0:T(8,128)(2,1)S(1)}, u32[]{:S(2)}, u32[]{:S(2)}) collective-permute-start(bf16[640,1024]{1,0:T(8,128)(2,1)S(1)} %collective-permute-done.own), channel_id=1, source_target_pairs={{0,1},{1,0},{2,3},{3,2},{4,5},{5,4},{6,7},{7,6}} | collective-permute-start | bytes 3932168 | tf_op jit(solution)/shard_map/ppermute | solution.py:576
  105.1 8.6 %collective-permute-start.2 = (bf16[128,1024]{1,0:T(8,128)(2,1)}, bf16[128,1024]{1,0:T(8,128)(2,1)S(1)}, u32[]{:S(2)}, u32[]{:S(2)}) collective-permute-start(bf16[128,1024]{1,0:T(8,128)(2,1)} %get-tuple-element.30), channel_id=1, source_target_pairs={{0,2},{2,0},{1,3},{3,1},{4,6},{6,4},{5,7},{7,5}} | collective-permute-start | bytes 786440 | tf_op jit(solution)/shard_map/ppermute | solution.py:572
  107.7 7.5 %copy-start.1 = (bf16[2,128,1024]{2,1,0:T(8,128)(2,1)S(1)}, bf16[2,128,1024]{2,1,0:T(8,128)(2,1)}, u32[]{:S(2)}) copy-start(bf16[2,128,1024]{2,1,0:T(8,128)(2,1)} %get-tuple-element.20.both) | copy-start | bytes 1572868
  113.7 1.5 %collective-permute-start.3 = (bf16[128,1024]{1,0:T(8,128)(2,1)S(1)}, bf16[128,1024]{1,0:T(8,128)(2,1)S(1)}, u32[]{:S(2)}, u32[]{:S(2)}) collective-permute-start(bf16[128,1024]{1,0:T(8,128)(2,1)S(1)} %collective-permute-done.2.own), channel_id=1, source_target_pairs={{0,1},{1,0},{2,3},{3,2},{4,5},{5,4},{6,7},{7,6}} | collective-permute-start | bytes 786440 | tf_op jit(solution)/shard_map/ppermute | solution.py:576

commit v2 on v1

--- a/solution.py
+++ b/solution.py
@@ -17,9 +17,12 @@
 HALF = D // 2
 RB = 256
 NB = ROWS // RB
-HB = RB // 2
-NX = 10
-PARTS = ((10, 15), (15, 16))
+HB = 64
+NP = ROWS // HB
+PER = RB // HB
+NX = 21
+LATE = {0: (12, 13), 1: (14,), 2: (15, 16), 3: (17, 18, 19, 20)}
+PARTS = ((21, 27), (27, 32))
 TILE = 512
 Q = 512
 NQ = HALF // Q
@@ -170,7 +173,7 @@
     def hidden(i, slot, t):
         cols = pl.ds(t * TILE, TILE)
         d_hidden = dot(dy_v[slot], wd_v[cols, :], ((1,), (1,)))
-        if isinstance(i, int) and t == 0:
+        if isinstance(i, int) and i == 0 and t == 0:
             wait(first_loads[1:])
         g, u = ga_v[slot, :, cols].astype(F32), up_v[slot, :, cols].astype(F32)
         sig = jax.nn.sigmoid(g)
@@ -185,90 +188,100 @@
         return dot(dgu_v[slot], wgu_v[wgu_at(half, t, size), :], ((1,), (1,)))
 
     def first_block():
+        halves = (1 - core, core)
+        pieces = [(n, half, q) for q in range(NQ) for n, half in enumerate(halves)]
+
+        def get(n):
+            wait(wgu_load(*pieces[n]))
+            return term(0, pieces[n][1], pieces[n][2], Q)
+
+        def give_up(q, got):
+            yours_0[q] = got.astype(BF16)
+            swap_0(q).start()
+
+        def take(q, got):
+            mine[:, pl.ds(q * Q, Q)] = got
+
+        def add_0(q):
+            swap_0(q).wait_recv()
+            s_0[q] = (mine[:, pl.ds(q * Q, Q)] + theirs_0[q].astype(F32)).astype(BF16)
+            cross_0(q).start()
+
         wait([first_loads[0], wd_load(0)])
         start([wd_load(2)])
         hidden(0, 0, 0)
+        start(wgu_load(*pieces[0]))
         wait([wd_load(1)])
-        halves = (1 - core, core)
-        order = [(n, half, q) for q in range(NQ) for n, half in enumerate(halves)]
-        start(wgu_load(*order[0]))
         hidden(0, 0, 1)
+        start(wgu_load(*pieces[1]))
         wait([wd_load(2)])
-        start(wgu_load(*order[1]))
-        start(wgu_load(*order[2]))
         hidden(0, 0, 2)
-
-        def add(q):
-            swap_0(q).wait_recv()
-            at = pl.ds(q * Q, Q)
-            s_0[q] = (mine[:, at] + theirs_0[q].astype(F32)).astype(BF16)
-            cross_0(q).start()
-
-        for at, (n, half, q) in enumerate(order):
-            wait(wgu_load(n, half, q))
-            if at + 3 < len(order):
-                start(wgu_load(*order[at + 3]))
-            elif at + 3 == len(order):
-                start(loads(1, 1))
-            elif at + 3 == len(order) + 1:
-                start(stores(0, 0))
-            got = term(0, half, q, Q)
-            if n == 0:
-                yours_0[q] = got.astype(BF16)
-                swap_0(q).start()
-            else:
-                mine[:, pl.ds(q * Q, Q)] = got
-                if q:
-                    add(q - 1)
-        add(NQ - 1)
+        start(loads(1, 1))
+        give_up(0, get(0))
+        start(wgu_load(*pieces[2]))
+        take(0, get(1))
+        start(wgu_load(*pieces[3]))
+        wait(loads(1, 1))
+        hidden(1, 1, 0)
+        add_0(0)
+        start(stores(0, 0))
+        hidden(1, 1, 1)
+        hidden(1, 1, 2)
+        give_up(1, get(2))
+        start(stores(1, 1))
+        start(loads(2, 0))
+        take(1, get(3))
+        add_0(1)
 
     def block(i):
         slot = lax.rem(i, 2)
-        wait(loads(i, slot))
-
-        @pl.when(i + 1 < NB)
-        def _():
-            start(loads(i + 1, 1 - slot))
+
+        @pl.when(i + 2 < NB)
+        def _():
+            start(loads(i + 2, slot))
 
         @pl.when(i == 1)
         def _():
             x_load(0).start()
-
-        @pl.when(i >= 2)
-        def _():
-            wait(stores(i - 2, slot))
-
-        for t in range(FF // TILE):
-            hidden(i, slot, t)
-        start(stores(i, slot))
 
         for t in range(HALF // TILE):
             yours[i, :, pl.ds(t * TILE, TILE)] = term(slot, 1 - core, t, TILE).astype(BF16)
         swap(i).start()
+
+        @pl.when(i + 1 < NB)
+        def _():
+            wait(loads(i + 1, 1 - slot))
+            wait(stores(i - 1, 1 - slot))
+            for t in range(FF // TILE):
+                hidden(i + 1, 1 - slot, t)
+            start(stores(i + 1, 1 - slot))
+
+        swap(i).wait_recv()
         for t in range(HALF // TILE):
-            mine[:, pl.ds(t * TILE, TILE)] = term(slot, core, t, TILE)
-        swap(i).wait_recv()
-        for n in range(2):
-            part = pl.ds(n * HB, HB)
-            s_v[2 * i + n] = (mine[part, :] + theirs[i, part, :].astype(F32)).astype(BF16)
-
-            @pl.when(2 * i + n < NX)
+            cols = pl.ds(t * TILE, TILE)
+            total = (term(slot, core, t, TILE) + theirs[i, :, cols].astype(F32)).astype(BF16)
+            for n in range(PER):
+                s_v[PER * i + n, :, cols] = total[n * HB : (n + 1) * HB]
+        for n in range(PER):
+
+            @pl.when(PER * i + n < NX)
             def _():
-                cross(2 * i + n).start()
-
-        for k in range(NX, 2 * NB):
-
-            @pl.when(i == k // 2)
+                cross(PER * i + n).start()
+
+        for k in range(NX, NP):
+
+            @pl.when(i == k // PER)
             def _():
                 start(hand_on(k))
 
-        @pl.when(i <= 2)
+        @pl.when(i <= NQ)
         def _():
             finish_0(i - 1)
 
         @pl.when(i >= 4)
         def _():
-            finish(i - 2)
+            finish(2 * i - 4)
+            finish(2 * i - 3)
 
     def step(i, carry):
         block(i)
@@ -279,19 +292,18 @@
 
     for j in range(1, NJ):
         x_load(j).start()
-    late = {0: (NB - 2,), 1: (NB - 1,), 3: tuple(range(NB, NX))}
     for j in range(NJ):
         x_load(j).wait()
         dw_at(j)[...] = dot(x_at(j)[...], dg_v[...], ((0,), (0,))).astype(BF16)
         dw_store(j).start()
-        for k in late.get(j, ()):
+        for k in LATE[j]:
             finish(k)
 
     for i in (NB - 2, NB - 1):
         wait(stores(i, i % 2))
     for i in range(1, NB):
         swap(i).wait_send()
-    for k in range(NX, 2 * NB):
+    for k in range(NX, NP):
         wait(hand_on(k))
     for j in range(NJ):
         dw_store(j).wait()
@@ -300,7 +312,7 @@
         cross_0(q).wait_send()
         keep_0(q).wait()
         give_0(q).wait()
-    for k in range(2, NX):
+    for k in range(PER, NX):
         cross(k).wait_send()
         keep(k).wait()
         give(k).wait()
@@ -309,7 +321,7 @@
 def terms(dy, gate, up, w_down, w_gate, w_up, x):
     hidden = jax.ShapeDtypeStruct((ROWS, FF), BF16)
     dma = pltpu.SemaphoreType.DMA
-    late = 2 * NB - NX
+    late = NP - NX
     return pl.pallas_call(
         term_kernel,
         name="terms",
@@ -336,7 +348,7 @@
             pltpu.VMEM((NB, RB, HALF), BF16),
             pltpu.VMEM((RB, HALF), F32),
             pltpu.VMEM((NB, RB, HALF), BF16),
-            pltpu.VMEM((2 * NB, HB, HALF), BF16),
+            pltpu.VMEM((NP, HB, HALF), BF16),
             pltpu.VMEM((NX, HB, HALF), BF16),
             pltpu.VMEM((NX, HB, HALF), BF16),
             *(pltpu.VMEM((NQ, RB, Q), BF16) for _ in range(5)),
@@ -503,36 +515,23 @@
     )(x, h, du, dy, dwg_t, dxp)
 
 
-def place_kernel(first, both, own, other, dx, out, both_v, own_v, other_v, out_v, in_sem, out_sem):
+def place_kernel(first, n, both, own, other, dx, out, out_v, sem):
     core = lax.rem(lax.axis_index("tp"), 2)
-    n = own.shape[0] // HB
-
-    def loads(k):
-        at = pl.ds(k * HB, HB)
-        return [
-            pltpu.make_async_copy(both.at[:, at], both_v.at[:, at], in_sem.at[0, k]),
-            pltpu.make_async_copy(own.at[at], own_v.at[at], in_sem.at[1, k]),
-            pltpu.make_async_copy(other.at[at], other_v.at[at], in_sem.at[2, k]),
-        ]
+    rows = own.shape[0] // n
 
     def store(k):
         return pltpu.make_async_copy(
-            out_v.at[pl.ds(k * HB, HB)], out.at[pl.ds((first + k) * HB, HB)], out_sem.at[k]
+            out_v.at[pl.ds(k * rows, rows)], out.at[pl.ds(first * HB + k * rows, rows)], sem.at[k]
         )
 
     for k in range(n):
-        for copy in loads(k):
-            copy.start()
-    for k in range(n):
-        at = pl.ds(k * HB, HB)
-        for copy in loads(k):
-            copy.wait()
+        at = pl.ds(k * rows, rows)
         for c in range(2):
 
             @pl.when(core == c)
             def _():
-                for half, q in ((c, own_v), (1 - c, other_v)):
-                    total = both_v[half, at].astype(F32) + q[at].astype(F32)
+                for half, q in ((c, own), (1 - c, other)):
+                    total = both[half, at].astype(F32) + q[at].astype(F32)
                     out_v[at, half * HALF : (half + 1) * HALF] = total.astype(BF16)
 
         store(k).start()
@@ -540,23 +539,16 @@
         store(k).wait()
 
 
-def place(dx, both, own, other, first):
+def place(dx, both, own, other, first, n):
     rows = own.shape[0]
-    n = rows // HB
+    near = pl.BlockSpec(memory_space=pltpu.VMEM)
     return pl.pallas_call(
-        functools.partial(place_kernel, first),
+        functools.partial(place_kernel, first, n),
         name="place",
         out_shape=jax.ShapeDtypeStruct(dx.shape, BF16),
-        in_specs=[ANY] * 4,
+        in_specs=[near, near, near, ANY],
         out_specs=ANY,
-        scratch_shapes=[
-            pltpu.VMEM((2, rows, HALF), BF16),
-            pltpu.VMEM((rows, HALF), BF16),
-            pltpu.VMEM((rows, HALF), BF16),
-            pltpu.VMEM((rows, D), BF16),
-            pltpu.SemaphoreType.DMA((3, n)),
-            pltpu.SemaphoreType.DMA((n,)),
-        ],
+        scratch_shapes=[pltpu.VMEM((rows, D), BF16), pltpu.SemaphoreType.DMA((n,))],
         input_output_aliases={3: 0},
         cost_estimate=pl.CostEstimate(flops=rows * D, bytes_accessed=rows * D * 6, transcendentals=0),
         compiler_params=pltpu.CompilerParams(vmem_limit_bytes=16 * MIB),
@@ -571,10 +563,12 @@
         for part in own:
             crossed.append(lax.ppermute(part, "tp", CHIPS))
         dw_gate, dw_up, dw_down, dx = weights(x, h, du, dy, dw_gate, dxp)
-        for (first, _), part, q in zip(PARTS, both, crossed):
-            dx, q = lax.optimization_barrier((dx, q))
-            near = lax.ppermute(q, "tp", CORES)
-            dx = place(dx, part, q, near, first)
+        dx, *crossed = lax.optimization_barrier((dx, *crossed))
+        near = []
+        for q in crossed:
+            near.append(lax.ppermute(q, "tp", CORES))
+        for n, (first, _) in enumerate(PARTS):
+            dx = place(dx, both[n], crossed[n], near[n], first, 2)
         return dx, dw_gate, dw_up, dw_down
 
     tokens, columns, rows = P("dp", None), P(None, "tp"), P("tp", None)

time: 117 us -> 114 us (0.974)
  waiting for transfers between devices: 6.48 us -> 1.93 us
    ppermute x2, waiting for transfers between devices: 3.8 us -> 0.15 us  [step(): crossed.append(lax.ppermute(part, 'tp', CHIPS))]
    pallas_call x1, Pallas kernels: 71.9 us -> 73.7 us  [terms(): pl.pallas_call(term_kernel, name='terms', out_shape=(hidden, hidden, jax....]
  transfers between devices with their start and end apart: 4 -> 4, of which waited for: 3 -> 2; matrix products, arithmetic and copies ran while one was open for 0% -> 0% of each run, Pallas kernels for 29% -> 29%
where the time goes in v2:
time: 114 us
  Pallas kernels  108 us (95%)
  starting transfers between devices  2.56 us (2%)
  waiting for transfers between devices  1.93 us (2%)
    pallas_call x1, Pallas kernels, terms(): pl.pallas_call(term_kernel, name='terms', out_shape=(hidden, hidden, jax....  73.7 us
    pallas_call x1, Pallas kernels, weights(): pl.pallas_call(weight_kernel, name='weights', grid=(2 * NJ,), out_shape=(...  31.9 us
    pallas_call x2, Pallas kernels, place(): pl.pallas_call(functools.partial(place_kernel, first, n), name='place', o...  2.55 us
  transfers between devices with their start and end apart: 4, of which 2 were waited for; matrix products, arithmetic and copies ran while one was open for 0% of the time, Pallas kernels for 29%

profile of v2, /device:TPU:0, one launch (start us, length us, event | category | flops | bytes accessed | tf_op | source)
XLA Modules:
  0.0 113.9 jit_solution(17445624971925057004)
XLA Ops:
  0.6 73.7 %terms.1 = (bf16[2048,1536]{1,0:T(8,128)(2,1)}, bf16[2048,1536]{1,0:T(8,128)(2,1)}, bf16[2048,1536]{1,0:T(8,128)(2,1)}, bf16[2,1344,1024]{2,1,0:T(8,128)(2,1)}, ...) custom-call(bf16[2048,2048]{1,0:T(8,128)(2,1)} %dy.3, ...), custom_call_target="tpu_custom_call" | custom-call | flops 51539607552 | bytes 62914560 | tf_op jit(solution)/shard_map/terms/pallas_call | solution.py:325
  74.3 0.3 collective-permute-start.1
  74.6 1.8 %collective-permute-start = (bf16[384,1024]{1,0:T(8,128)(2,1)}, bf16[384,1024]{1,0:T(8,128)(2,1)S(1)}, u32[]{:S(2)}, u32[]{:S(2)}) collective-permute-start(bf16[384,1024]{1,0:T(8,128)(2,1)} %get-tuple-element.25), channel_id=1, source_target_pairs={{0,2},{2,0},{1,3},{3,1},{4,6},{6,4},{5,7},{7,5}} | collective-permute-start | bytes 2359304 | tf_op jit(solution)/shard_map/ppermute | solution.py:564
  76.4 0.0 copy-start
  76.4 31.9 %weights.1 = (bf16[2048,1536]{1,0:T(8,128)(2,1)}, bf16[2048,1536]{1,0:T(8,128)(2,1)}, bf16[1536,2048]{1,0:T(8,128)(2,1)}, bf16[2048,2048]{1,0:T(8,128)(2,1)}) custom-call(bf16[2048,2048]{1,0:T(8,128)(2,1)} %x.3, bf16[2048,1536]{1,0:T(8,128)(2,1)} %get-tuple-element.20.h, bf16[2048,1536]{1,0:T(8,128)(2,1)} %get-tuple-element.21.du, bf16[2048,2048]{1,0:T(8,128)(2,1)} %dy.3, ...), custom_call_target="tpu_custom_call" | custom-call | flops 25769803776 | bytes 62914560 | tf_op jit(solution)/shard_map/weights/pallas_call | solution.py:483
  108.2 0.0 collective-permute-done.1.own
  108.3 0.1 collective-permute-done.own
  108.4 0.0 collective-permute-start.3
  108.4 0.5 collective-permute-start.2
  108.9 1.8 %collective-permute-done.3.other = bf16[384,1024]{1,0:T(8,128)(2,1)S(1)} collective-permute-done((bf16[384,1024]{1,0:T(8,128)(2,1)S(1)}, bf16[384,1024]{1,0:T(8,128)(2,1)S(1)}, u32[]{:S(2)}, u32[]{:S(2)}) %collective-permute-start.3) | collective-permute-done | bytes 786464 | tf_op jit(solution)/shard_map/ppermute | solution.py:569
  110.7 0.0 copy-done
  110.7 0.0 copy-start.1
  110.7 1.3 %place.2.dx = bf16[2048,2048]{1,0:T(8,128)(2,1)} custom-call(bf16[2,384,1024]{2,1,0:T(8,128)(2,1)S(1)} %copy-done, bf16[384,1024]{1,0:T(8,128)(2,1)S(1)} %collective-permute-done.own, bf16[384,1024]{1,0:T(8,128)(2,1)S(1)} %collective-permute-done.3.other, bf16[2048,2048]{1,0:T(8,128)(2,1)} %get-tuple-element.30.dx), custom_call_target="tpu_custom_call", output_to_operand_aliasing={{}: (3, {})} | custom-call | flops 786432 | bytes 4718592 | tf_op jit(solution)/shard_map/place/pallas_call | solution.py:545
  112.0 0.0 collective-permute-done.2.other
  112.0 0.4 copy-done.1
  112.5 1.2 %place.3 = bf16[2048,2048]{1,0:T(8,128)(2,1)} custom-call(bf16[2,320,1024]{2,1,0:T(8,128)(2,1)S(1)} %copy-done.1, bf16[320,1024]{1,0:T(8,128)(2,1)S(1)} %collective-permute-done.1.own, bf16[320,1024]{1,0:T(8,128)(2,1)S(1)} %collective-permute-done.2.other, bf16[2048,2048]{1,0:T(8,128)(2,1)} %place.2.dx), custom_call_target="tpu_custom_call", output_to_operand_aliasing={{}: (3, {})} | custom-call | flops 655360 | bytes 3932160 | tf_op jit(solution)/shard_map/place/pallas_call | solution.py:545
Async XLA Ops:
  74.3 33.9 %collective-permute-start.1 = (bf16[320,1024]{1,0:T(8,128)(2,1)}, bf16[320,1024]{1,0:T(8,128)(2,1)S(1)}, u32[]{:S(2)}, u32[]{:S(2)}) collective-permute-start(bf16[320,1024]{1,0:T(8,128)(2,1)} %get-tuple-element.26), channel_id=1, source_target_pairs={{0,2},{2,0},{1,3},{3,1},{4,6},{6,4},{5,7},{7,5}} | collective-permute-start | bytes 1966088 | tf_op jit(solution)/shard_map/ppermute | solution.py:564
  74.6 33.8 %collective-permute-start = (bf16[384,1024]{1,0:T(8,128)(2,1)}, bf16[384,1024]{1,0:T(8,128)(2,1)S(1)}, u32[]{:S(2)}, u32[]{:S(2)}) collective-permute-start(bf16[384,1024]{1,0:T(8,128)(2,1)} %get-tuple-element.25), channel_id=1, source_target_pairs={{0,2},{2,0},{1,3},{3,1},{4,6},{6,4},{5,7},{7,5}} | collective-permute-start | bytes 2359304 | tf_op jit(solution)/shard_map/ppermute | solution.py:564
  76.4 34.3 %copy-start = (bf16[2,384,1024]{2,1,0:T(8,128)(2,1)S(1)}, bf16[2,384,1024]{2,1,0:T(8,128)(2,1)}, u32[]{:S(2)}) copy-start(bf16[2,384,1024]{2,1,0:T(8,128)(2,1)} %get-tuple-element.28.both) | copy-start | bytes 4718596
  108.4 2.3 %collective-permute-start.3 = (bf16[384,1024]{1,0:T(8,128)(2,1)S(1)}, bf16[384,1024]{1,0:T(8,128)(2,1)S(1)}, u32[]{:S(2)}, u32[]{:S(2)}) collective-permute-start(bf16[384,1024]{1,0:T(8,128)(2,1)S(1)} %collective-permute-done.own), channel_id=1, source_target_pairs={{0,1},{1,0},{2,3},{3,2},{4,5},{5,4},{6,7},{7,6}} | collective-permute-start | bytes 2359304 | tf_op jit(solution)/shard_map/ppermute | solution.py:569
  108.4 3.6 %collective-permute-start.2 = (bf16[320,1024]{1,0:T(8,128)(2,1)S(1)}, bf16[320,1024]{1,0:T(8,128)(2,1)S(1)}, u32[]{:S(2)}, u32[]{:S(2)}) collective-permute-start(bf16[320,1024]{1,0:T(8,128)(2,1)S(1)} %collective-permute-done.1.own), channel_id=1, source_target_pairs={{0,1},{1,0},{2,3},{3,2},{4,5},{5,4},{6,7},{7,6}} | collective-permute-start | bytes 1966088 | tf_op jit(solution)/shard_map/ppermute | solution.py:569
  110.7 1.8 %copy-start.1 = (bf16[2,320,1024]{2,1,0:T(8,128)(2,1)S(1)}, bf16[2,320,1024]{2,1,0:T(8,128)(2,1)}, u32[]{:S(2)}) copy-start(bf16[2,320,1024]{2,1,0:T(8,128)(2,1)} %get-tuple-element.19.both) | copy-start | bytes 3932164

commit v3 on v2

--- a/solution.py
+++ b/solution.py
@@ -22,13 +22,14 @@
 PER = RB // HB
 NX = 21
 LATE = {0: (12, 13), 1: (14,), 2: (15, 16), 3: (17, 18, 19, 20)}
-PARTS = ((21, 27), (27, 32))
+PARTS = ((21, 25), (25, 32))
 TILE = 512
 Q = 512
 NQ = HALF // Q
 BX = 512
 NJ = D // BX
-BH = FF // NJ
+BH = 512
+NK = FF // BH
 
 CHIPS = [(0, 2), (2, 0), (1, 3), (3, 1)]
 CORES = [(0, 1), (1, 0), (2, 3), (3, 2)]
@@ -469,12 +470,13 @@
         od_v[slot] = dot(h_v[:, pl.ds(pl.multiple_of(k * BH, BH), BH)], dy_v[...], ((0,), (0,))).astype(BF16)
         put_down(k, slot).start()
 
-    @pl.when(j == 2 * NJ - 1)
+    @pl.when(j == NJ + NK - 1)
     def _():
         for copy in puts:
             copy.wait()
         for k in (NJ - 2, NJ - 1):
             put_up(k, k % 2).wait()
+        for k in (NK - 2, NK - 1):
             put_down(k, k % 2).wait()
 
 
@@ -483,7 +485,7 @@
     return pl.pallas_call(
         weight_kernel,
         name="weights",
-        grid=(2 * NJ,),
+        grid=(NJ + NK,),
         out_shape=(
             jax.ShapeDtypeStruct((D, FF), BF16),
             jax.ShapeDtypeStruct((D, FF), BF16),
@@ -511,7 +513,7 @@
             dma((2,)),
         ],
         cost_estimate=pl.CostEstimate(flops=4 * ROWS * D * FF, bytes_accessed=60 * MIB, transcendentals=0),
-        compiler_params=pltpu.CompilerParams(vmem_limit_bytes=60 * MIB),
+        compiler_params=pltpu.CompilerParams(vmem_limit_bytes=52 * MIB),
     )(x, h, du, dy, dwg_t, dxp)
 
 

time: 114 us -> 115 us (level)
  transfers between devices with their start and end apart: 4 -> 4, of which waited for: 2 -> 2; matrix products, arithmetic and copies ran while one was open for 0% -> 0% of each run, Pallas kernels for 29% -> 28%
where the time goes in v3:
time: 115 us
  Pallas kernels  108 us (94%)
  waiting for transfers between devices  3 us (3%)
  starting transfers between devices  2.56 us (2%)
    pallas_call x1, Pallas kernels, terms(): pl.pallas_call(term_kernel, name='terms', out_shape=(hidden, hidden, jax....  73.7 us
    pallas_call x1, Pallas kernels, weights(): pl.pallas_call(weight_kernel, name='weights', grid=(NJ + NK,), out_shape=...  31.7 us
    ppermute x2, waiting for transfers between devices, step(): near.append(lax.ppermute(q, 'tp', CORES))  2.71 us
    pallas_call x2, Pallas kernels, place(): pl.pallas_call(functools.partial(place_kernel, first, n), name='place', o...  2.55 us
  transfers between devices with their start and end apart: 4, of which 2 were waited for; matrix products, arithmetic and copies ran while one was open for 0% of the time, Pallas kernels for 28%

profile of v3, /device:TPU:0, one launch (start us, length us, event | category | flops | bytes accessed | tf_op | source)
XLA Modules:
  0.0 115.2 jit_solution(14681453581078800374)
XLA Ops:
  0.6 73.7 %terms.1 = (bf16[2048,1536]{1,0:T(8,128)(2,1)}, bf16[2048,1536]{1,0:T(8,128)(2,1)}, bf16[2048,1536]{1,0:T(8,128)(2,1)}, bf16[2,1344,1024]{2,1,0:T(8,128)(2,1)}, ...) custom-call(bf16[2048,2048]{1,0:T(8,128)(2,1)} %dy.3, ...), custom_call_target="tpu_custom_call" | custom-call | flops 51539607552 | bytes 62914560 | tf_op jit(solution)/shard_map/terms/pallas_call | solution.py:326
  74.3 0.3 collective-permute-start
  74.6 1.8 %collective-permute-start.1 = (bf16[448,1024]{1,0:T(8,128)(2,1)}, bf16[448,1024]{1,0:T(8,128)(2,1)S(1)}, u32[]{:S(2)}, u32[]{:S(2)}) collective-permute-start(bf16[448,1024]{1,0:T(8,128)(2,1)} %get-tuple-element.26), channel_id=1, source_target_pairs={{0,2},{2,0},{1,3},{3,1},{4,6},{6,4},{5,7},{7,5}} | collective-permute-start | bytes 2752520 | tf_op jit(solution)/shard_map/ppermute | solution.py:566
  76.4 0.0 copy-start.1
  76.4 31.7 %weights.1 = (bf16[2048,1536]{1,0:T(8,128)(2,1)}, bf16[2048,1536]{1,0:T(8,128)(2,1)}, bf16[1536,2048]{1,0:T(8,128)(2,1)}, bf16[2048,2048]{1,0:T(8,128)(2,1)}) custom-call(bf16[2048,2048]{1,0:T(8,128)(2,1)} %x.3, bf16[2048,1536]{1,0:T(8,128)(2,1)} %get-tuple-element.20.h, bf16[2048,1536]{1,0:T(8,128)(2,1)} %get-tuple-element.21.du, bf16[2048,2048]{1,0:T(8,128)(2,1)} %dy.3, ...), custom_call_target="tpu_custom_call" | custom-call | flops 25769803776 | bytes 62914560 | tf_op jit(solution)/shard_map/weights/pallas_call | solution.py:485
  108.1 0.0 collective-permute-done.own
  108.1 0.3 collective-permute-done.1.own
  108.4 0.0 collective-permute-start.2
  108.4 0.5 collective-permute-start.3
  108.9 2.7 %collective-permute-done.3.other = bf16[256,1024]{1,0:T(8,128)(2,1)S(1)} collective-permute-done((bf16[256,1024]{1,0:T(8,128)(2,1)S(1)}, bf16[256,1024]{1,0:T(8,128)(2,1)S(1)}, u32[]{:S(2)}, u32[]{:S(2)}) %collective-permute-start.3) | collective-permute-done | bytes 524320 | tf_op jit(solution)/shard_map/ppermute | solution.py:571
  111.6 0.0 copy-done.1
  111.6 0.0 copy-start
  111.6 1.1 place.2.dx
  112.7 0.0 collective-permute-done.2.other
  112.8 0.8 copy-done
  113.5 1.5 %place.3 = bf16[2048,2048]{1,0:T(8,128)(2,1)} custom-call(bf16[2,448,1024]{2,1,0:T(8,128)(2,1)S(1)} %copy-done, bf16[448,1024]{1,0:T(8,128)(2,1)S(1)} %collective-permute-done.1.own, bf16[448,1024]{1,0:T(8,128)(2,1)S(1)} %collective-permute-done.2.other, bf16[2048,2048]{1,0:T(8,128)(2,1)} %place.2.dx), custom_call_target="tpu_custom_call", output_to_operand_aliasing={{}: (3, {})} | custom-call | flops 917504 | bytes 5505024 | tf_op jit(solution)/shard_map/place/pallas_call | solution.py:547
Async XLA Ops:
  74.3 33.8 %collective-permute-start = (bf16[256,1024]{1,0:T(8,128)(2,1)}, bf16[256,1024]{1,0:T(8,128)(2,1)S(1)}, u32[]{:S(2)}, u32[]{:S(2)}) collective-permute-start(bf16[256,1024]{1,0:T(8,128)(2,1)} %get-tuple-element.25), channel_id=1, source_target_pairs={{0,2},{2,0},{1,3},{3,1},{4,6},{6,4},{5,7},{7,5}} | collective-permute-start | bytes 1572872 | tf_op jit(solution)/shard_map/ppermute | solution.py:566
  74.6 33.8 %collective-permute-start.1 = (bf16[448,1024]{1,0:T(8,128)(2,1)}, bf16[448,1024]{1,0:T(8,128)(2,1)S(1)}, u32[]{:S(2)}, u32[]{:S(2)}) collective-permute-start(bf16[448,1024]{1,0:T(8,128)(2,1)} %get-tuple-element.26), channel_id=1, source_target_pairs={{0,2},{2,0},{1,3},{3,1},{4,6},{6,4},{5,7},{7,5}} | collective-permute-start | bytes 2752520 | tf_op jit(solution)/shard_map/ppermute | solution.py:566
  76.4 35.3 %copy-start.1 = (bf16[2,256,1024]{2,1,0:T(8,128)(2,1)S(1)}, bf16[2,256,1024]{2,1,0:T(8,128)(2,1)}, u32[]{:S(2)}) copy-start(bf16[2,256,1024]{2,1,0:T(8,128)(2,1)} %get-tuple-element.28.both) | copy-start | bytes 3145732
  108.4 4.3 %collective-permute-start.2 = (bf16[448,1024]{1,0:T(8,128)(2,1)S(1)}, bf16[448,1024]{1,0:T(8,128)(2,1)S(1)}, u32[]{:S(2)}, u32[]{:S(2)}) collective-permute-start(bf16[448,1024]{1,0:T(8,128)(2,1)S(1)} %collective-permute-done.1.own), channel_id=1, source_target_pairs={{0,1},{1,0},{2,3},{3,2},{4,5},{5,4},{6,7},{7,6}} | collective-permute-start | bytes 2752520 | tf_op jit(solution)/shard_map/ppermute | solution.py:571
  108.4 3.2 %collective-permute-start.3 = (bf16[256,1024]{1,0:T(8,128)(2,1)S(1)}, bf16[256,1024]{1,0:T(8,128)(2,1)S(1)}, u32[]{:S(2)}, u32[]{:S(2)}) collective-permute-start(bf16[256,1024]{1,0:T(8,128)(2,1)S(1)} %collective-permute-done.own), channel_id=1, source_target_pairs={{0,1},{1,0},{2,3},{3,2},{4,5},{5,4},{6,7},{7,6}} | collective-permute-start | bytes 1572872 | tf_op jit(solution)/shard_map/ppermute | solution.py:571
  111.6 1.9 %copy-start = (bf16[2,448,1024]{2,1,0:T(8,128)(2,1)S(1)}, bf16[2,448,1024]{2,1,0:T(8,128)(2,1)}, u32[]{:S(2)}) copy-start(bf16[2,448,1024]{2,1,0:T(8,128)(2,1)} %get-tuple-element.19.both) | copy-start | bytes 5505028
